TPU v7x, 512 devices: a whole 4x4x16 slice. The times are simulated.
512 devices in a mesh: pts: 32 (over x, y, core), cand: 16 (over z).
Axes of the slice: x: 4, y: 4, z: 16, core: 2. Of those that a mesh axis runs over, the one named last changes fastest.
Arguments:
- points: bfloat16 [32768, 1024], P('pts'), may hold values from -6 to 6
- weights: float32 [32768], P('pts'), may hold values from 0.5 to 5
- coverage: float32 [32768], P('pts'), may hold values from -0.5 to 1
- candidates: bfloat16 [16384, 1024], P('cand'), may hold values from -6 to 6
- picks: int32 [64], replicated, may hold values from 0 to 16383
Outputs:
- gains: float32 [16384], P('cand')
- top_gains: float32 [64], replicated
- new_coverage: float32 [32768], P('pts')
All inputs are finite; a program needn't handle non-finite values.
Results may differ from a plain program's by a relative error of at most 0.0003.
Values may be sent and summed in bfloat16 or wider, within the bound.
No kernel may reach another device: no remote copies, remote signals or barrier semaphores. Data moves between devices by JAX's collectives and lax.ppermute only.
A program may use at most 64 MiB of HBM per device.

v0:
```python
import jax
import jax.numpy as jnp
from jax import lax
from jax.sharding import PartitionSpec as P

TOPK = 64


def from_everyone(x, axis):
    copies = jnp.broadcast_to(x, (lax.axis_size(axis), *x.shape))
    return lax.all_to_all(copies, axis, split_axis=0, concat_axis=0, tiled=True)


def over_copies(x, axis):
    return from_everyone(x, axis).sum(axis=0)


def combined_pairwise(pieces, combine):
    while len(jax.tree.leaves(pieces)[0]) > 1:
        pieces = jax.vmap(combine)(*(pieces[side::2] for side in (0, 1)))
    return pieces[0]


def joined_all(x, axis, combine):
    pieces = from_everyone(x, axis)
    return combined_pairwise(pieces, combine)


def taken_together(x, axis):
    return from_everyone(x, axis).max(axis=0)


def best_values(first, second):
    return lax.top_k(jnp.concatenate([first, second]), TOPK)[0]


def on_device(points, weights, coverage, candidates, picks):
    scale = points.shape[1] ** (-0.5)
    total = points.shape[0] * lax.axis_size("pts")
    cand_rows = candidates.shape[0]
    offset = lax.axis_index("cand") * cand_rows
    sims = jnp.dot(points, candidates.T, preferred_element_type=jnp.float32) * scale
    partial_value = (
        jnp.sum(weights[:, None] * jnp.maximum(sims - coverage[:, None], 0.0), axis=0) / total
    )
    gains = over_copies(partial_value, "pts")
    top_gains = joined_all(lax.top_k(gains, TOPK)[0], "cand", best_values)
    columns = offset + jnp.arange(cand_rows, dtype=jnp.int32)
    chosen = jnp.any(picks[:, None] == columns[None, :], axis=0)
    local_best = jnp.max(jnp.where(chosen[None, :], sims, -1e30), axis=1)
    best_sim = taken_together(local_best, "cand")
    new_coverage = jnp.maximum(coverage, best_sim)
    return (gains, top_gains, new_coverage)


def solution(mesh):
    placed = (P("pts", None), P("pts"), P("pts"), P("cand", None), P())
    return jax.shard_map(
        on_device, mesh=mesh, in_specs=placed, out_specs=(P("cand"), P(), P("pts")), check_vma=False
    )
```

profile of v0, /device:TPU:1, one launch (start us, length us, event | category | flops | bytes accessed | tf_op | source)
XLA Modules:
  0.0 69.8 jit_solution(17755846284915081702)
XLA Ops:
  0.6 0.0 copy-start
  0.7 0.9 %compare_reduce_fusion = pred[1024]{0:T(1024)(128)(4,1)S(1)} fusion(s32[1024]{0:T(1024)S(1)} %iota_add_fusion, s32[64]{0:T(128)} %param.9), kind=kLoop, calls=%fused_computation.2 | loop fusion | flops 130048 | bytes 5376 | tf_op jit(solution)/shard_map/reduce_or | solution.py:49
  1.6 0.7 copy-done
  2.2 0.0 copy-start.2
  2.2 4.4 %select_reduce_fusion = (f32[1024]{0:T(1024)S(1)}, f32[1024]{0:T(1024)S(1)}) fusion(pred[1024]{0:T(1024)(128)(4,1)S(1)} %compare_reduce_fusion, f32[1024]{0:T(1024)} %param.7, f32[1024]{0:T(1024)} %param.6, bf16[1024,1024]{1,0:T(8,128)(2,1)S(1)} %copy-done, bf16[1024,1024]{1,0:T(8,128)(2,1)} %param.8), kind=kOutput, calls=%fused_computation | convolution fusion | flops 2154821632 | bytes 4211712 | tf_op jit(solution)/shard_map/dot_general | solution.py:42
  6.6 0.1 broadcast_in_dim.26
  6.7 17.3 %all_to_all.21 = f32[32,1,1024]{2,1,0:T(1,128)S(1)} all-to-all(f32[32,1,1024]{2,1,0:T(1,128)S(1)} %broadcast_in_dim.26), channel_id=1, replica_groups=mesh['pts'=32,'cand'=16] {'pts'}, dimensions={0} | all-to-all | bytes 262144 | tf_op jit(solution)/shard_map/all_to_all | solution.py:11
  23.9 0.1 reduce_sum.19
  24.0 0.0 copy-start.1
  24.1 4.4 %top_k.36 = (f32[1024]{0:T(1024)S(1)}, s32[1024]{0:T(1024)}) sort(f32[1024]{0:T(1024)S(1)} %reduce_sum.19, s32[1024]{0:T(1024)S(1)} %iota.20), dimensions={0}, to_apply=%region_2.0 | sort | flops 10240 | bytes 16384 | tf_op jit(solution)/shard_map/top_k | solution.py:47
  28.5 24.8 %all_to_all.22 = f32[16,1,64]{2,1,0:T(1,128)S(1)} all-to-all(f32[16,1,64]{2,1,0:T(1,128)S(1)} %broadcast_in_dim.27), channel_id=1, replica_groups=mesh['pts'=32,'cand'=16] {'cand'}, dimensions={0} | all-to-all | bytes 8192 | tf_op jit(solution)/shard_map/all_to_all | solution.py:11
  53.3 0.7 broadcast_in_dim.30
  54.0 3.5 %all-to-all-start.2 = ((f32[16,1,1024]{2,1,0:T(1,128)}), f32[16,1,1024]{2,1,0:T(1,128)S(1)}, u32[]{:S(2)}, u32[]{:S(2)}) async-start(f32[16,1,1024]{2,1,0:T(1,128)} %broadcast_in_dim.30), calls=%async_computation.2 | async-start | bytes 131072 | tf_op jit(solution)/shard_map/all_to_all | solution.py:11
  57.5 0.1 pad_maximum_fusion
  57.6 2.6 %top_k.38 = (f32[8,128]{1,0:T(8,128)S(1)}, s32[8,128]{1,0:T(8,128)}) sort(f32[8,128]{1,0:T(8,128)S(1)} %pad_maximum_fusion, s32[8,128]{1,0:T(8,128)S(1)} %iota.21), dimensions={1}, to_apply=%region_3.4 | sort | flops 10240 | bytes 16384 | tf_op jit(solution)/shard_map/vmap()/top_k | solution.py:34
  60.3 0.1 pad_maximum_fusion.1
  60.4 2.6 %top_k.44 = (f32[4,128]{1,0:T(4,128)S(1)}, s32[4,128]{1,0:T(4,128)}) sort(f32[4,128]{1,0:T(4,128)S(1)} %pad_maximum_fusion.1, s32[4,128]{1,0:T(4,128)S(1)} %iota.22), dimensions={1}, to_apply=%region_4.5 | sort | flops 4608 | bytes 8192 | tf_op jit(solution)/shard_map/vmap()/top_k | solution.py:34
  63.0 0.1 pad_maximum_fusion.2
  63.1 2.6 %top_k.46 = (f32[2,128]{1,0:T(2,128)S(1)}, s32[2,128]{1,0:T(2,128)}) sort(f32[2,128]{1,0:T(2,128)S(1)} %pad_maximum_fusion.2, s32[2,128]{1,0:T(2,128)S(1)} %iota.23), dimensions={1}, to_apply=%region_5.6 | sort | flops 2048 | bytes 4096 | tf_op jit(solution)/shard_map/vmap()/top_k | solution.py:34
  65.7 0.1 pad_maximum_fusion.3
  65.8 2.6 %top_k.47 = (f32[1,128]{1,0:T(1,128)S(1)}, s32[1,128]{1,0:T(1,128)}) sort(f32[1,128]{1,0:T(1,128)S(1)} %pad_maximum_fusion.3, s32[1,128]{1,0:T(1,128)S(1)} %iota.24), dimensions={1}, to_apply=%region_6.7 | sort | flops 896 | bytes 2048 | tf_op jit(solution)/shard_map/vmap()/top_k | solution.py:34
  68.4 0.5 slice_bitcast_fusion
  68.9 0.2 all-to-all-done.2
  69.1 0.1 reduce_max.19
  69.2 0.0 copy-done.2
  69.2 0.6 max.11
  69.8 0.0 copy-done.1
  (16 shorter events, 0.2 us)
Async XLA Ops:
  0.6 1.6 %copy-start = (bf16[1024,1024]{1,0:T(8,128)(2,1)S(1)}, bf16[1024,1024]{1,0:T(8,128)(2,1)}, u32[]{:S(2)}) copy-start(bf16[1024,1024]{1,0:T(8,128)(2,1)} %param.5) | copy-start | bytes 6291460
  2.2 66.9 %copy-start.2 = (f32[1024]{0:T(1024)S(1)}, f32[1024]{0:T(1024)}, u32[]{:S(2)}) copy-start(f32[1024]{0:T(1024)} %param.7) | copy-start | bytes 12292
  24.0 45.7 %copy-start.1 = (f32[1024]{0:T(1024)}, f32[1024]{0:T(1024)S(1)}, u32[]{:S(2)}) copy-start(f32[1024]{0:T(1024)S(1)} %reduce_sum.19) | copy-start | bytes 12292
  54.0 15.1 %all-to-all-start.2 = ((f32[16,1,1024]{2,1,0:T(1,128)}), f32[16,1,1024]{2,1,0:T(1,128)S(1)}, u32[]{:S(2)}, u32[]{:S(2)}) async-start(f32[16,1,1024]{2,1,0:T(1,128)} %broadcast_in_dim.30), calls=%async_computation.2 | async-start | bytes 131072 | tf_op jit(solution)/shard_map/all_to_all | solution.py:11
where the time goes:
time: 70.6 us; the launch traced here: 69.8 us
  blocking collectives  42.1 us (60%)
  other arithmetic  16.8 us (24%)
  matrix products  4.35 us (6%)
  starting transfers between devices  3.5 us (5%)
  local copies, waits for them, and re-layouts  2.06 us (3%)
  between operations  0.71 us (1%)
    all_to_all x2, blocking collectives, from_everyone(): return lax.all_to_all(copies, axis, split_axis=0, concat_axis=0, tiled=True)  42.1 us
    top_k x4, other arithmetic, best_values(): return lax.top_k(jnp.concatenate([first, second]), TOPK)[0]  10.4 us
    top_k x1, other arithmetic, on_device(): top_gains = joined_all(lax.top_k(gains, TOPK)[0], 'cand', best_values)  4.43 us
    dot_general x1, matrix products, on_device(): jnp.dot(points, candidates.T, preferred_element_type=jnp.float32) * scale  4.35 us
    all_to_all x1, starting transfers between devices, from_everyone(): return lax.all_to_all(copies, axis, split_axis=0, concat_axis=0, tiled=True)  3.5 us
  transfers between devices with their start and end apart: 1, of which 1 were waited for; matrix products, arithmetic and copies ran while one was open for 16% of the time, Pallas kernels for 0%

commit v1 on v0

v1 whole, which is shorter than its diff:
```python
import functools

import jax
import jax.numpy as jnp
from jax import lax
from jax.experimental import pallas as pl
from jax.experimental.pallas import tpu as pltpu
from jax.sharding import PartitionSpec as P

TOPK = 64
LANES = 128
FAR = -1e30


def column_blocks(rows):
    turned = rows.T
    return [
        jnp.broadcast_to(turned[:, s : s + 1], (LANES, LANES)) for s in range(rows.shape[0])
    ]


def descending(values):
    n = values.shape[0]
    above = [jnp.zeros((8, LANES), jnp.float32) for _ in range(n)]
    for block in column_blocks(values):
        for r in range(n):
            larger = jnp.where(block > values[r : r + 1, :], 1.0, 0.0)
            above[r] = above[r] + larger.reshape(LANES // 8, 8, LANES).sum(axis=0)
    place = lax.broadcasted_iota(jnp.int32, (LANES, LANES), 0).astype(jnp.float32)
    best = jnp.full((LANES, LANES), jnp.inf, jnp.float32)
    for r in range(n):
        count = above[r].sum(axis=0, keepdims=True)
        best = jnp.minimum(best, jnp.where(count <= place, values[r : r + 1, :], jnp.inf))
    return best.T.min(axis=0, keepdims=True)


def scores_kernel(
    scale, total, n_pts, offset_ref, picks_ref, weights_ref, coverage_ref, points_hbm, cands_hbm,
    gains_ref, best_ref, points, cands, cover_cols, weight_cols, sems,
):
    chunks = points.shape[0] // 256
    parts = cands.shape[0] // 256

    def fetch(src, dst, i, sem):
        return pltpu.make_async_copy(
            src.at[pl.ds(i * 256, 256), :], dst.at[pl.ds(i * 256, 256), :], sem
        )

    point_copies = [fetch(points_hbm, points, i, sems.at[i]) for i in range(chunks)]
    cand_copies = [fetch(cands_hbm, cands, i, sems.at[chunks + i]) for i in range(parts)]
    for copy in [point_copies[0], *cand_copies, *point_copies[1:]]:
        copy.start()

    for s, block in enumerate(column_blocks(coverage_ref[...] * (1.0 / scale))):
        cover_cols[s * LANES : (s + 1) * LANES, :] = block
    for s, block in enumerate(column_blocks(weights_ref[...] * (scale / total))):
        weight_cols[s * LANES : (s + 1) * LANES, :] = block
    rows = cands.shape[0] // LANES
    mine = (
        offset_ref[0]
        + lax.broadcasted_iota(jnp.int32, (rows, LANES), 0) * LANES
        + lax.broadcasted_iota(jnp.int32, (rows, LANES), 1)
    )
    chosen = mine == picks_ref[0]
    for k in range(1, picks_ref.shape[0]):
        chosen = jnp.logical_or(chosen, mine == picks_ref[k])
    barred = jnp.where(chosen, 0.0, FAR)

    sums = [jnp.zeros((8, LANES), jnp.float32) for _ in range(rows)]
    for i in range(chunks):
        point_copies[i].wait()
        block = points[i * 256 : (i + 1) * 256, :]
        cover = cover_cols[i * 256 : (i + 1) * 256, :]
        weight = weight_cols[i * 256 : (i + 1) * 256, :]
        best = jnp.full((256, LANES), FAR, jnp.float32)
        for j in range(parts):
            if i == 0:
                cand_copies[j].wait()
            sims = lax.dot_general(
                block, cands[j * 256 : (j + 1) * 256, :], (((1,), (1,)), ((), ())),
                preferred_element_type=jnp.float32,
            )
            for h in range(2):
                r = 2 * j + h
                part = sims[:, h * LANES : (h + 1) * LANES]
                value = jnp.maximum(part - cover, 0.0) * weight
                sums[r] = sums[r] + value.reshape(32, 8, LANES).sum(axis=0)
                best = jnp.maximum(best, part + barred[r : r + 1, :])
        for h in range(2):
            turned = best[h * LANES : (h + 1) * LANES, :].T
            best_ref[0:1, (2 * i + h) * LANES : (2 * i + h + 1) * LANES] = (
                turned.max(axis=0, keepdims=True) * scale
            )
    gains = jnp.concatenate([s.sum(axis=0, keepdims=True) for s in sums], axis=0)
    gains_ref[...] = jnp.broadcast_to(gains[None], (n_pts, rows, LANES))


def gather_kernel(n_cand, partial_ref, best_ref, gains_ref, out_ref):
    gains = partial_ref[...].sum(axis=0)
    gains_ref[...] = gains
    top = descending(gains)
    for i in range(n_cand):
        out_ref[i, :, 0:LANES] = top
        out_ref[i, :, LANES:] = best_ref[...]


def final_kernel(all_ref, coverage_ref, gains_ref, gains_out, top_out, coverage_out):
    gains_out[...] = gains_ref[...]
    n = all_ref.shape[0]
    best = all_ref[0, :, LANES:]
    for i in range(1, n):
        best = jnp.maximum(best, all_ref[i, :, LANES:])
    coverage_out[...] = jnp.maximum(coverage_ref[...], best)
    even = jnp.concatenate([all_ref[i, :, 0:LANES] for i in range(0, n, 2)], axis=0)
    odd = jnp.concatenate([all_ref[i, :, 0:LANES] for i in range(1, n, 2)], axis=0)
    lane = lax.broadcasted_iota(jnp.int32, even.shape, 1)
    tops = jnp.where(lane < TOPK, even, pltpu.roll(odd, TOPK, 1))
    top_out[...] = descending(tops)[:, 0:TOPK]


def on_device(points, weights, coverage, candidates, picks):
    n_pts, n_cand = lax.axis_size("pts"), lax.axis_size("cand")
    local, width = points.shape
    cand_rows = candidates.shape[0]
    scale = width ** (-0.5)
    offset = (lax.axis_index("cand") * cand_rows).astype(jnp.int32).reshape(1)
    rows = cand_rows // LANES
    vmem = pl.BlockSpec(memory_space=pltpu.VMEM)
    smem = pl.BlockSpec(memory_space=pltpu.SMEM)
    hbm = pl.BlockSpec(memory_space=pltpu.HBM)
    f32 = jnp.float32

    partial, best = pl.pallas_call(
        functools.partial(scores_kernel, scale, float(local * n_pts), n_pts),
        out_shape=(
            jax.ShapeDtypeStruct((n_pts, rows, LANES), f32),
            jax.ShapeDtypeStruct((1, local), f32),
        ),
        in_specs=[smem, smem, vmem, vmem, hbm, hbm],
        out_specs=(vmem, vmem),
        scratch_shapes=[
            pltpu.VMEM(points.shape, points.dtype),
            pltpu.VMEM(candidates.shape, candidates.dtype),
            pltpu.VMEM((local, LANES), f32),
            pltpu.VMEM((local, LANES), f32),
            pltpu.SemaphoreType.DMA((local // 256 + cand_rows // 256,)),
        ],
        compiler_params=pltpu.CompilerParams(vmem_limit_bytes=24 * 1024 * 1024),
        cost_estimate=pl.CostEstimate(
            flops=2 * local * cand_rows * width, bytes_accessed=4 * 1024 * 1024, transcendentals=0
        ),
    )(
        offset,
        *(
            pltpu.with_memory_space_constraint(x, pltpu.HBM)
            for x in (
                picks, weights.reshape(-1, LANES), coverage.reshape(-1, LANES), points, candidates
            )
        ),
    )

    partial = lax.all_to_all(partial, "pts", split_axis=0, concat_axis=0, tiled=True)

    gains, message = pl.pallas_call(
        functools.partial(gather_kernel, n_cand),
        out_shape=(
            jax.ShapeDtypeStruct((rows, LANES), f32),
            jax.ShapeDtypeStruct((n_cand, 1, LANES + local), f32),
        ),
        in_specs=[vmem, vmem],
        out_specs=(vmem, vmem),
        compiler_params=pltpu.CompilerParams(vmem_limit_bytes=8 * 1024 * 1024),
    )(partial, best)

    message = lax.all_to_all(message, "cand", split_axis=0, concat_axis=0, tiled=True)

    gains, top_gains, new_coverage = pl.pallas_call(
        final_kernel,
        out_shape=(
            jax.ShapeDtypeStruct((rows, LANES), f32),
            jax.ShapeDtypeStruct((1, TOPK), f32),
            jax.ShapeDtypeStruct((1, local), f32),
        ),
        in_specs=[vmem, vmem, vmem],
        out_specs=(vmem, vmem, vmem),
        compiler_params=pltpu.CompilerParams(vmem_limit_bytes=8 * 1024 * 1024),
    )(message, coverage.reshape(1, -1), gains)
    return gains.reshape(-1), top_gains.reshape(-1), new_coverage.reshape(-1)


def solution(mesh):
    placed = (P("pts", None), P("pts"), P("pts"), P("cand", None), P())
    return jax.shard_map(
        on_device, mesh=mesh, in_specs=placed, out_specs=(P("cand"), P(), P("pts")), check_vma=False
    )
```

time: 70.6 us -> 52.5 us (0.74)
  other arithmetic: 16.8 us -> 0 us
  Pallas kernels: 0 us -> 9.14 us
  matrix products: 4.35 us -> 0 us
  starting transfers between devices: 3.5 us -> 0 us
  local copies, waits for them, and re-layouts: 2.06 us -> 0.01 us
    top_k x5 -> x0, other arithmetic: 14.9 us -> none  [the longest x4 10.4 us: best_values(): return lax.top_k(jnp.concatenate([first, second]), TOPK)[0]]
    pallas_call x0 -> x3, Pallas kernels: none -> 9.14 us  [the longest x1 7.08 us: on_device(): pl.pallas_call(functools.partial(scores_kernel, scale, float(local * n_pt...]
    dot_general x1 -> x0, matrix products: 4.35 us -> none  [on_device(): jnp.dot(points, candidates.T, preferred_element_type=jnp.float32) * scale]
    all_to_all x1 -> x0, starting transfers between devices: 3.5 us -> none  [from_everyone(): return lax.all_to_all(copies, axis, split_axis=0, concat_axis=0, tiled=True)]
    reduce_or x1 -> x0, other arithmetic: 0.92 us -> none  [on_device(): chosen = jnp.any(picks[:, None] == columns[None, :], axis=0)]
    broadcast_in_dim x3 -> x0, local copies, waits for them, and re-layouts: 0.73 us -> none  [from_everyone(): copies = jnp.broadcast_to(x, (lax.axis_size(axis), *x.shape))]
  transfers between devices with their start and end apart: 1 -> 0, of which waited for: 1 -> 0; matrix products, arithmetic and copies ran while one was open for 16% -> 0% of each run, Pallas kernels for 0% -> 0%
where the time goes in v1:
time: 52.5 us; the launch traced here: 52.3 us
  blocking collectives  42.5 us (81%)
  Pallas kernels  9.14 us (17%)
  between operations  0.66 us (1%)
    all_to_all x1, blocking collectives, on_device(): lax.all_to_all(message, 'cand', split_axis=0, concat_axis=0, tiled=True)  25.2 us
    all_to_all x1, blocking collectives, on_device(): lax.all_to_all(partial, 'pts', split_axis=0, concat_axis=0, tiled=True)  17.3 us
    pallas_call x1, Pallas kernels, on_device(): pl.pallas_call(functools.partial(scores_kernel, scale, float(local * n_pt...  7.08 us
    pallas_call x1, Pallas kernels, on_device(): pl.pallas_call(final_kernel, out_shape=(jax.ShapeDtypeStruct((rows, LANES...  1.35 us

profile of v1, /device:TPU:1, one launch (start us, length us, event | category | flops | bytes accessed | tf_op | source)
XLA Modules:
  0.0 52.3 jit_solution(5845971303676894046)
XLA Ops:
  0.6 0.0 copy-start
  0.6 7.1 %shard_map.76 = (f32[32,8,128]{2,1,0:T(8,128)S(1)}, f32[1,1024]{1,0:T(1,128)S(1)}) custom-call(s32[1]{0:T(128)} %bitcast.offset_ref, s32[64]{0:T(128)} %picks_ref.1, f32[8,128]{1,0:T(8,128)} %bitcast.9, f32[8,128]{1,0:T(8,128)} %bitcast.7, bf16[1024,1024]{1,0:T(8,128)(2,1)} %points_hbm.1, bf16[1024,1024]{1,0:T(8,128)(2,1)} %cands_hbm.1), custom_call_target="tpu_custom_call" | custom-call | flops 2147483648 | bytes 4194304 | tf_op jit(solution)/shard_map/pallas_call | solution.py:133
  7.7 17.3 %all_to_all.10.partial_ref = f32[32,8,128]{2,1,0:T(8,128)S(1)} all-to-all(f32[32,8,128]{2,1,0:T(8,128)S(1)} %get-tuple-element.10), channel_id=1, replica_groups=mesh['pts'=32,'cand'=16] {'pts'}, dimensions={0} | all-to-all | bytes 262144 | tf_op jit(solution)/shard_map/all_to_all | solution.py:162
  25.0 0.7 %shard_map.77 = (f32[8,128]{1,0:T(8,128)S(1)}, f32[16,1,1152]{2,1,0:T(1,128)S(1)}) custom-call(f32[32,8,128]{2,1,0:T(8,128)S(1)} %all_to_all.10.partial_ref, f32[1,1024]{1,0:T(1,128)S(1)} %get-tuple-element.11.best_ref), custom_call_target="tpu_custom_call" | custom-call | tf_op jit(solution)/shard_map/pallas_call | solution.py:164
  25.7 25.2 %all_to_all.11.all_ref = f32[16,1,1152]{2,1,0:T(1,128)S(1)} all-to-all(f32[16,1,1152]{2,1,0:T(1,128)S(1)} %get-tuple-element.12), channel_id=1, replica_groups=mesh['pts'=32,'cand'=16] {'cand'}, dimensions={0} | all-to-all | bytes 147456 | tf_op jit(solution)/shard_map/all_to_all | solution.py:175
  50.9 0.0 copy-done
  50.9 1.4 %shard_map.78 = (f32[8,128]{1,0:T(8,128)}, f32[1,64]{1,0:T(1,128)}, f32[1,1024]{1,0:T(1,128)}) custom-call(f32[16,1,1152]{2,1,0:T(1,128)S(1)} %all_to_all.11.all_ref, f32[1,1024]{1,0:T(1,128)S(1)} %bitcast.8, f32[8,128]{1,0:T(8,128)S(1)} %get-tuple-element.13.gains_ref), custom_call_target="tpu_custom_call" | custom-call | tf_op jit(solution)/shard_map/pallas_call | solution.py:177
Async XLA Ops:
  0.6 50.3 %copy-start = (f32[1024]{0:T(1024)S(1)}, f32[1024]{0:T(1024)}, u32[]{:S(2)}) copy-start(f32[1024]{0:T(1024)} %param.7) | copy-start | bytes 12292

commit v2 on v1

--- a/solution.py
+++ b/solution.py
@@ -35,64 +35,55 @@
 
 
 def scores_kernel(
-    scale, total, n_pts, offset_ref, picks_ref, weights_ref, coverage_ref, points_hbm, cands_hbm,
-    gains_ref, best_ref, points, cands, cover_cols, weight_cols, sems,
+    scale, total, n_pts, picks_hbm, weights_hbm, coverage_hbm, points_hbm, cands_hbm,
+    gains_ref, best_ref, points, cands, cover_cols, weight_cols, picks, weights, coverage, sems,
 ):
-    chunks = points.shape[0] // 256
-    parts = cands.shape[0] // 256
-
-    def fetch(src, dst, i, sem):
-        return pltpu.make_async_copy(
-            src.at[pl.ds(i * 256, 256), :], dst.at[pl.ds(i * 256, 256), :], sem
-        )
-
-    point_copies = [fetch(points_hbm, points, i, sems.at[i]) for i in range(chunks)]
-    cand_copies = [fetch(cands_hbm, cands, i, sems.at[chunks + i]) for i in range(parts)]
-    for copy in [point_copies[0], *cand_copies, *point_copies[1:]]:
+    operands = (
+        (picks_hbm, picks), (weights_hbm, weights), (coverage_hbm, coverage),
+        (points_hbm, points), (cands_hbm, cands),
+    )
+    copies = [
+        pltpu.make_async_copy(src, dst, sems.at[i]) for i, (src, dst) in enumerate(operands)
+    ]
+    for copy in copies:
         copy.start()
 
-    for s, block in enumerate(column_blocks(coverage_ref[...] * (1.0 / scale))):
+    for copy in copies[:3]:
+        copy.wait()
+    for s, block in enumerate(column_blocks(coverage[...] * (1.0 / scale))):
         cover_cols[s * LANES : (s + 1) * LANES, :] = block
-    for s, block in enumerate(column_blocks(weights_ref[...] * (scale / total))):
+    for s, block in enumerate(column_blocks(weights[...] * (scale / total))):
         weight_cols[s * LANES : (s + 1) * LANES, :] = block
-    rows = cands.shape[0] // LANES
+    local, rows = points.shape[0], cands.shape[0] // LANES
     mine = (
-        offset_ref[0]
+        lax.axis_index("cand") * cands.shape[0]
         + lax.broadcasted_iota(jnp.int32, (rows, LANES), 0) * LANES
         + lax.broadcasted_iota(jnp.int32, (rows, LANES), 1)
     )
-    chosen = mine == picks_ref[0]
-    for k in range(1, picks_ref.shape[0]):
-        chosen = jnp.logical_or(chosen, mine == picks_ref[k])
+    chosen = mine == picks[0]
+    for k in range(1, picks.shape[0]):
+        chosen = jnp.logical_or(chosen, mine == picks[k])
     barred = jnp.where(chosen, 0.0, FAR)
 
-    sums = [jnp.zeros((8, LANES), jnp.float32) for _ in range(rows)]
-    for i in range(chunks):
-        point_copies[i].wait()
-        block = points[i * 256 : (i + 1) * 256, :]
-        cover = cover_cols[i * 256 : (i + 1) * 256, :]
-        weight = weight_cols[i * 256 : (i + 1) * 256, :]
-        best = jnp.full((256, LANES), FAR, jnp.float32)
-        for j in range(parts):
-            if i == 0:
-                cand_copies[j].wait()
-            sims = lax.dot_general(
-                block, cands[j * 256 : (j + 1) * 256, :], (((1,), (1,)), ((), ())),
-                preferred_element_type=jnp.float32,
-            )
-            for h in range(2):
-                r = 2 * j + h
-                part = sims[:, h * LANES : (h + 1) * LANES]
-                value = jnp.maximum(part - cover, 0.0) * weight
-                sums[r] = sums[r] + value.reshape(32, 8, LANES).sum(axis=0)
-                best = jnp.maximum(best, part + barred[r : r + 1, :])
+    for copy in copies[3:]:
+        copy.wait()
+    sums = []
+    best = None
+    for j in range(0, rows, 2):
+        sims = lax.dot_general(
+            points[...], cands[j * LANES : (j + 2) * LANES, :], (((1,), (1,)), ((), ())),
+            preferred_element_type=jnp.float32,
+        )
         for h in range(2):
-            turned = best[h * LANES : (h + 1) * LANES, :].T
-            best_ref[0:1, (2 * i + h) * LANES : (2 * i + h + 1) * LANES] = (
-                turned.max(axis=0, keepdims=True) * scale
-            )
-    gains = jnp.concatenate([s.sum(axis=0, keepdims=True) for s in sums], axis=0)
-    gains_ref[...] = jnp.broadcast_to(gains[None], (n_pts, rows, LANES))
+            part = sims[:, h * LANES : (h + 1) * LANES]
+            value = jnp.maximum(part - cover_cols[...], 0.0) * weight_cols[...]
+            sums.append(value.reshape(local // 8, 8, LANES).sum(axis=0).sum(axis=0, keepdims=True))
+            part = part + barred[j + h : j + h + 1, :]
+            best = part if best is None else jnp.maximum(best, part)
+    for r in range(0, local, LANES):
+        turned = best[r : r + LANES, :].T
+        best_ref[0:1, r : r + LANES] = turned.max(axis=0, keepdims=True) * scale
+    gains_ref[...] = jnp.broadcast_to(jnp.concatenate(sums, axis=0)[None], (n_pts, rows, LANES))
 
 
 def gather_kernel(n_cand, partial_ref, best_ref, gains_ref, out_ref):
@@ -123,10 +114,8 @@
     local, width = points.shape
     cand_rows = candidates.shape[0]
     scale = width ** (-0.5)
-    offset = (lax.axis_index("cand") * cand_rows).astype(jnp.int32).reshape(1)
     rows = cand_rows // LANES
     vmem = pl.BlockSpec(memory_space=pltpu.VMEM)
-    smem = pl.BlockSpec(memory_space=pltpu.SMEM)
     hbm = pl.BlockSpec(memory_space=pltpu.HBM)
     f32 = jnp.float32
 
@@ -136,21 +125,23 @@
             jax.ShapeDtypeStruct((n_pts, rows, LANES), f32),
             jax.ShapeDtypeStruct((1, local), f32),
         ),
-        in_specs=[smem, smem, vmem, vmem, hbm, hbm],
+        in_specs=[hbm] * 5,
         out_specs=(vmem, vmem),
         scratch_shapes=[
             pltpu.VMEM(points.shape, points.dtype),
             pltpu.VMEM(candidates.shape, candidates.dtype),
             pltpu.VMEM((local, LANES), f32),
             pltpu.VMEM((local, LANES), f32),
-            pltpu.SemaphoreType.DMA((local // 256 + cand_rows // 256,)),
+            pltpu.SMEM(picks.shape, picks.dtype),
+            pltpu.VMEM((local // LANES, LANES), f32),
+            pltpu.VMEM((local // LANES, LANES), f32),
+            pltpu.SemaphoreType.DMA((5,)),
         ],
         compiler_params=pltpu.CompilerParams(vmem_limit_bytes=24 * 1024 * 1024),
         cost_estimate=pl.CostEstimate(
             flops=2 * local * cand_rows * width, bytes_accessed=4 * 1024 * 1024, transcendentals=0
         ),
     )(
-        offset,
         *(
             pltpu.with_memory_space_constraint(x, pltpu.HBM)
             for x in (

time: 52.5 us -> 50.3 us (0.958)
  Pallas kernels: 9.14 us -> 7.01 us
    pallas_call x1, Pallas kernels: 7.08 us -> 4.94 us  [on_device(): pl.pallas_call(functools.partial(scores_kernel, scale, float(local * n_pt...]
where the time goes in v2:
time: 50.3 us; the launch traced here: 50.2 us
  blocking collectives  42.5 us (84%)
  Pallas kernels  7.01 us (14%)
  between operations  0.66 us (1%)
    all_to_all x1, blocking collectives, on_device(): lax.all_to_all(message, 'cand', split_axis=0, concat_axis=0, tiled=True)  25.2 us
    all_to_all x1, blocking collectives, on_device(): lax.all_to_all(partial, 'pts', split_axis=0, concat_axis=0, tiled=True)  17.3 us
    pallas_call x1, Pallas kernels, on_device(): pl.pallas_call(functools.partial(scores_kernel, scale, float(local * n_pt...  4.94 us
    pallas_call x1, Pallas kernels, on_device(): pl.pallas_call(final_kernel, out_shape=(jax.ShapeDtypeStruct((rows, LANES...  1.35 us

profile of v2, /device:TPU:1, one launch (start us, length us, event | category | flops | bytes accessed | tf_op | source)
XLA Modules:
  0.0 50.2 jit_solution(9233208421147751885)
XLA Ops:
  0.6 0.0 copy-start
  0.6 4.9 %shard_map.76 = (f32[32,8,128]{2,1,0:T(8,128)S(1)}, f32[1,1024]{1,0:T(1,128)S(1)}) custom-call(s32[64]{0:T(128)} %picks_hbm.1, f32[8,128]{1,0:T(8,128)} %bitcast.8, f32[8,128]{1,0:T(8,128)} %bitcast.6, bf16[1024,1024]{1,0:T(8,128)(2,1)} %points_hbm.1, bf16[1024,1024]{1,0:T(8,128)(2,1)} %cands_hbm.1), custom_call_target="tpu_custom_call" | custom-call | flops 2147483648 | bytes 4194304 | tf_op jit(solution)/shard_map/pallas_call | solution.py:122
  5.6 17.3 %all_to_all.10.partial_ref = f32[32,8,128]{2,1,0:T(8,128)S(1)} all-to-all(f32[32,8,128]{2,1,0:T(8,128)S(1)} %get-tuple-element.10), channel_id=1, replica_groups=mesh['pts'=32,'cand'=16] {'pts'}, dimensions={0} | all-to-all | bytes 262144 | tf_op jit(solution)/shard_map/all_to_all | solution.py:153
  22.9 0.7 %shard_map.77 = (f32[8,128]{1,0:T(8,128)S(1)}, f32[16,1,1152]{2,1,0:T(1,128)S(1)}) custom-call(f32[32,8,128]{2,1,0:T(8,128)S(1)} %all_to_all.10.partial_ref, f32[1,1024]{1,0:T(1,128)S(1)} %get-tuple-element.11.best_ref), custom_call_target="tpu_custom_call" | custom-call | tf_op jit(solution)/shard_map/pallas_call | solution.py:155
  23.6 25.2 %all_to_all.11.all_ref = f32[16,1,1152]{2,1,0:T(1,128)S(1)} all-to-all(f32[16,1,1152]{2,1,0:T(1,128)S(1)} %get-tuple-element.12), channel_id=1, replica_groups=mesh['pts'=32,'cand'=16] {'cand'}, dimensions={0} | all-to-all | bytes 147456 | tf_op jit(solution)/shard_map/all_to_all | solution.py:166
  48.8 0.0 copy-done
  48.8 1.4 %shard_map.78 = (f32[8,128]{1,0:T(8,128)}, f32[1,64]{1,0:T(1,128)}, f32[1,1024]{1,0:T(1,128)}) custom-call(f32[16,1,1152]{2,1,0:T(1,128)S(1)} %all_to_all.11.all_ref, f32[1,1024]{1,0:T(1,128)S(1)} %bitcast.7, f32[8,128]{1,0:T(8,128)S(1)} %get-tuple-element.13.gains_ref), custom_call_target="tpu_custom_call" | custom-call | tf_op jit(solution)/shard_map/pallas_call | solution.py:168
Async XLA Ops:
  0.6 48.2 %copy-start = (f32[1024]{0:T(1024)S(1)}, f32[1024]{0:T(1024)}, u32[]{:S(2)}) copy-start(f32[1024]{0:T(1024)} %param.7) | copy-start | bytes 12292

commit v3 on v2

--- a/solution.py
+++ b/solution.py
@@ -10,6 +10,8 @@
 TOPK = 64
 LANES = 128
 FAR = -1e30
+FIRST_PTS = 21
+FIRST_CAND = 11
 
 
 def column_blocks(rows):
@@ -109,6 +111,14 @@
     top_out[...] = descending(tops)[:, 0:TOPK]
 
 
+def exchanged(x, axis, first):
+    n = lax.axis_size(axis)
+    members = [[(first + i) % n for i in range(n)]]
+    return lax.all_to_all(
+        x, axis, split_axis=0, concat_axis=0, axis_index_groups=members, tiled=True
+    )
+
+
 def on_device(points, weights, coverage, candidates, picks):
     n_pts, n_cand = lax.axis_size("pts"), lax.axis_size("cand")
     local, width = points.shape
@@ -150,7 +160,7 @@
         ),
     )
 
-    partial = lax.all_to_all(partial, "pts", split_axis=0, concat_axis=0, tiled=True)
+    partial = exchanged(partial, "pts", FIRST_PTS)
 
     gains, message = pl.pallas_call(
         functools.partial(gather_kernel, n_cand),
@@ -163,7 +173,7 @@
         compiler_params=pltpu.CompilerParams(vmem_limit_bytes=8 * 1024 * 1024),
     )(partial, best)
 
-    message = lax.all_to_all(message, "cand", split_axis=0, concat_axis=0, tiled=True)
+    message = exchanged(message, "cand", FIRST_CAND)
 
     gains, top_gains, new_coverage = pl.pallas_call(
         final_kernel,

time: 50.3 us -> 42 us (0.83)
  blocking collectives: 42.5 us -> 34.1 us
    all_to_all x2, blocking collectives: 42.5 us -> 34.1 us  [exchanged(): lax.all_to_all(x, axis, split_axis=0, concat_axis=0, axis_index_groups=me...]
where the time goes in v3:
time: 42 us; the launch traced here: 41.8 us
  blocking collectives  34.1 us (81%)
  Pallas kernels  7.01 us (17%)
  between operations  0.66 us (2%)
    all_to_all x2, blocking collectives, exchanged(): lax.all_to_all(x, axis, split_axis=0, concat_axis=0, axis_index_groups=me...  34.1 us
    pallas_call x1, Pallas kernels, on_device(): pl.pallas_call(functools.partial(scores_kernel, scale, float(local * n_pt...  4.94 us
    pallas_call x1, Pallas kernels, on_device(): pl.pallas_call(final_kernel, out_shape=(jax.ShapeDtypeStruct((rows, LANES...  1.35 us

profile of v3, /device:TPU:1, one launch (start us, length us, event | category | flops | bytes accessed | tf_op | source)
XLA Modules:
  0.0 41.8 jit_solution(2148875146793615367)
XLA Ops:
  0.6 0.0 copy-start
  0.6 4.9 %shard_map.76 = (f32[32,8,128]{2,1,0:T(8,128)S(1)}, f32[1,1024]{1,0:T(1,128)S(1)}) custom-call(s32[64]{0:T(128)} %picks_hbm.1, f32[8,128]{1,0:T(8,128)} %bitcast.8, f32[8,128]{1,0:T(8,128)} %bitcast.6, bf16[1024,1024]{1,0:T(8,128)(2,1)} %points_hbm.1, bf16[1024,1024]{1,0:T(8,128)(2,1)} %cands_hbm.1), custom_call_target="tpu_custom_call" | custom-call | flops 2147483648 | bytes 4194304 | tf_op jit(solution)/shard_map/pallas_call | solution.py:132
  5.6 16.1 %all_to_all.10.partial_ref = f32[32,8,128]{2,1,0:T(8,128)S(1)} all-to-all(f32[32,8,128]{2,1,0:T(8,128)S(1)} %get-tuple-element.10), channel_id=1, replica_groups={{336,352,368,384,400,416,432,448,464,480,496,0,16,32,48,64,80,96,112,12..., dimensions={0} | all-to-all | bytes 262144 | tf_op jit(solution)/shard_map/all_to_all | solution.py:117
  21.7 0.7 %shard_map.77 = (f32[8,128]{1,0:T(8,128)S(1)}, f32[16,1,1152]{2,1,0:T(1,128)S(1)}) custom-call(f32[32,8,128]{2,1,0:T(8,128)S(1)} %all_to_all.10.partial_ref, f32[1,1024]{1,0:T(1,128)S(1)} %get-tuple-element.11.best_ref), custom_call_target="tpu_custom_call" | custom-call | tf_op jit(solution)/shard_map/pallas_call | solution.py:165
  22.5 18.0 %all_to_all.11.all_ref = f32[16,1,1152]{2,1,0:T(1,128)S(1)} all-to-all(f32[16,1,1152]{2,1,0:T(1,128)S(1)} %get-tuple-element.12), channel_id=1, replica_groups={{11,12,13,14,15,0,1,2,3,4,5,6,7,8,9,10},{27,28,29,30,31,16,17,18,19,20,..., dimensions={0} | all-to-all | bytes 147456 | tf_op jit(solution)/shard_map/all_to_all | solution.py:117
  40.4 0.0 copy-done
  40.4 1.4 %shard_map.78 = (f32[8,128]{1,0:T(8,128)}, f32[1,64]{1,0:T(1,128)}, f32[1,1024]{1,0:T(1,128)}) custom-call(f32[16,1,1152]{2,1,0:T(1,128)S(1)} %all_to_all.11.all_ref, f32[1,1024]{1,0:T(1,128)S(1)} %bitcast.7, f32[8,128]{1,0:T(8,128)S(1)} %get-tuple-element.13.gains_ref), custom_call_target="tpu_custom_call" | custom-call | tf_op jit(solution)/shard_map/pallas_call | solution.py:178
Async XLA Ops:
  0.6 39.8 %copy-start = (f32[1024]{0:T(1024)S(1)}, f32[1024]{0:T(1024)}, u32[]{:S(2)}) copy-start(f32[1024]{0:T(1024)} %param.7) | copy-start | bytes 12292

commit v4 on v3

--- a/solution.py
+++ b/solution.py
@@ -21,14 +21,13 @@
     ]
 
 
-def descending(values):
+def ranked(values, place):
     n = values.shape[0]
     above = [jnp.zeros((8, LANES), jnp.float32) for _ in range(n)]
     for block in column_blocks(values):
         for r in range(n):
             larger = jnp.where(block > values[r : r + 1, :], 1.0, 0.0)
             above[r] = above[r] + larger.reshape(LANES // 8, 8, LANES).sum(axis=0)
-    place = lax.broadcasted_iota(jnp.int32, (LANES, LANES), 0).astype(jnp.float32)
     best = jnp.full((LANES, LANES), jnp.inf, jnp.float32)
     for r in range(n):
         count = above[r].sum(axis=0, keepdims=True)
@@ -69,29 +68,42 @@
 
     for copy in copies[3:]:
         copy.wait()
-    sums = []
-    best = None
+    sums = [jnp.zeros((8, LANES), jnp.float32) for _ in range(rows)]
+    half = local // 2
+    best = [None, None]
     for j in range(0, rows, 2):
-        sims = lax.dot_general(
-            points[...], cands[j * LANES : (j + 2) * LANES, :], (((1,), (1,)), ((), ())),
-            preferred_element_type=jnp.float32,
-        )
-        for h in range(2):
-            part = sims[:, h * LANES : (h + 1) * LANES]
-            value = jnp.maximum(part - cover_cols[...], 0.0) * weight_cols[...]
-            sums.append(value.reshape(local // 8, 8, LANES).sum(axis=0).sum(axis=0, keepdims=True))
-            part = part + barred[j + h : j + h + 1, :]
-            best = part if best is None else jnp.maximum(best, part)
-    for r in range(0, local, LANES):
-        turned = best[r : r + LANES, :].T
-        best_ref[0:1, r : r + LANES] = turned.max(axis=0, keepdims=True) * scale
+        last = j == rows - 2
+        for first, size in ((0, half), (half, half)) if last else ((0, local),):
+            span = slice(first, first + size)
+            sims = lax.dot_general(
+                points[span, :], cands[j * LANES : (j + 2) * LANES, :], (((1,), (1,)), ((), ())),
+                preferred_element_type=jnp.float32,
+            )
+            masked = None
+            for h in range(2):
+                part = sims[:, h * LANES : (h + 1) * LANES]
+                value = jnp.maximum(part - cover_cols[span, :], 0.0) * weight_cols[span, :]
+                sums[j + h] = sums[j + h] + value.reshape(size // 8, 8, LANES).sum(axis=0)
+                part = part + barred[j + h : j + h + 1, :]
+                masked = part if masked is None else jnp.maximum(masked, part)
+            for q in range(first // half, (first + size) // half):
+                piece = masked[q * half - first : (q + 1) * half - first, :]
+                best[q] = piece if best[q] is None else jnp.maximum(best[q], piece)
+                for r in range(0, half if last else 0, LANES):
+                    turned = best[q][r : r + LANES, :].T
+                    best_ref[0:1, q * half + r : q * half + r + LANES] = (
+                        turned.max(axis=0, keepdims=True) * scale
+                    )
+    sums = [s.sum(axis=0, keepdims=True) for s in sums]
     gains_ref[...] = jnp.broadcast_to(jnp.concatenate(sums, axis=0)[None], (n_pts, rows, LANES))
 
 
 def gather_kernel(n_cand, partial_ref, best_ref, gains_ref, out_ref):
     gains = partial_ref[...].sum(axis=0)
     gains_ref[...] = gains
-    top = descending(gains)
+    row = lax.broadcasted_iota(jnp.int32, (LANES, LANES), 0)
+    falling = lax.axis_index("cand") % 2 == 0
+    top = ranked(gains, jnp.where(falling, row, TOPK - 1 - row).astype(jnp.float32))
     for i in range(n_cand):
         out_ref[i, :, 0:LANES] = top
         out_ref[i, :, LANES:] = best_ref[...]
@@ -104,11 +116,14 @@
     for i in range(1, n):
         best = jnp.maximum(best, all_ref[i, :, LANES:])
     coverage_out[...] = jnp.maximum(coverage_ref[...], best)
-    even = jnp.concatenate([all_ref[i, :, 0:LANES] for i in range(0, n, 2)], axis=0)
-    odd = jnp.concatenate([all_ref[i, :, 0:LANES] for i in range(1, n, 2)], axis=0)
-    lane = lax.broadcasted_iota(jnp.int32, even.shape, 1)
-    tops = jnp.where(lane < TOPK, even, pltpu.roll(odd, TOPK, 1))
-    top_out[...] = descending(tops)[:, 0:TOPK]
+    pairs = [
+        jnp.maximum(all_ref[i, :, 0:LANES], all_ref[i + 1, :, 0:LANES]) for i in range(0, n, 2)
+    ]
+    left, right = (jnp.concatenate(half, axis=0) for half in (pairs[0::2], pairs[1::2]))
+    lane = lax.broadcasted_iota(jnp.int32, left.shape, 1)
+    tops = jnp.where(lane < TOPK, left, pltpu.roll(right, TOPK, 1))
+    place = lax.broadcasted_iota(jnp.int32, (LANES, LANES), 0).astype(jnp.float32)
+    top_out[...] = ranked(tops, place)[:, 0:TOPK]
 
 
 def exchanged(x, axis, first):

time: 42 us -> 41.6 us (level)
  no operation moved by 1% of the time
where the time goes in v4:
time: 41.6 us; the launch traced here: 41.4 us
  blocking collectives  34.1 us (82%)
  Pallas kernels  6.65 us (16%)
  between operations  0.66 us (2%)
    all_to_all x2, blocking collectives, exchanged(): lax.all_to_all(x, axis, split_axis=0, concat_axis=0, axis_index_groups=me...  34.1 us
    pallas_call x1, Pallas kernels, on_device(): pl.pallas_call(functools.partial(scores_kernel, scale, float(local * n_pt...  4.88 us
    pallas_call x1, Pallas kernels, on_device(): pl.pallas_call(final_kernel, out_shape=(jax.ShapeDtypeStruct((rows, LANES...  1.06 us

profile of v4, /device:TPU:1, one launch (start us, length us, event | category | flops | bytes accessed | tf_op | source)
XLA Modules:
  0.0 41.4 jit_solution(10011558808941129065)
XLA Ops:
  0.6 0.0 copy-start
  0.6 4.9 %shard_map.76 = (f32[32,8,128]{2,1,0:T(8,128)S(1)}, f32[1,1024]{1,0:T(1,128)S(1)}) custom-call(s32[64]{0:T(128)} %picks_hbm.1, f32[8,128]{1,0:T(8,128)} %bitcast.8, f32[8,128]{1,0:T(8,128)} %bitcast.6, bf16[1024,1024]{1,0:T(8,128)(2,1)} %points_hbm.1, bf16[1024,1024]{1,0:T(8,128)(2,1)} %cands_hbm.1), custom_call_target="tpu_custom_call" | custom-call | flops 2147483648 | bytes 4194304 | tf_op jit(solution)/shard_map/pallas_call | solution.py:147
  5.5 16.1 %all_to_all.10.partial_ref = f32[32,8,128]{2,1,0:T(8,128)S(1)} all-to-all(f32[32,8,128]{2,1,0:T(8,128)S(1)} %get-tuple-element.10), channel_id=1, replica_groups={{336,352,368,384,400,416,432,448,464,480,496,0,16,32,48,64,80,96,112,12..., dimensions={0} | all-to-all | bytes 262144 | tf_op jit(solution)/shard_map/all_to_all | solution.py:132
  21.7 0.7 %shard_map.77 = (f32[8,128]{1,0:T(8,128)S(1)}, f32[16,1,1152]{2,1,0:T(1,128)S(1)}) custom-call(f32[32,8,128]{2,1,0:T(8,128)S(1)} %all_to_all.10.partial_ref, f32[1,1024]{1,0:T(1,128)S(1)} %get-tuple-element.11.best_ref), custom_call_target="tpu_custom_call" | custom-call | tf_op jit(solution)/shard_map/pallas_call | solution.py:180
  22.4 18.0 %all_to_all.11.all_ref = f32[16,1,1152]{2,1,0:T(1,128)S(1)} all-to-all(f32[16,1,1152]{2,1,0:T(1,128)S(1)} %get-tuple-element.12), channel_id=1, replica_groups={{11,12,13,14,15,0,1,2,3,4,5,6,7,8,9,10},{27,28,29,30,31,16,17,18,19,20,..., dimensions={0} | all-to-all | bytes 147456 | tf_op jit(solution)/shard_map/all_to_all | solution.py:132
  40.4 0.0 copy-done
  40.4 1.1 %shard_map.78 = (f32[8,128]{1,0:T(8,128)}, f32[1,64]{1,0:T(1,128)}, f32[1,1024]{1,0:T(1,128)}) custom-call(f32[16,1,1152]{2,1,0:T(1,128)S(1)} %all_to_all.11.all_ref, f32[1,1024]{1,0:T(1,128)S(1)} %bitcast.7, f32[8,128]{1,0:T(8,128)S(1)} %get-tuple-element.13.gains_ref), custom_call_target="tpu_custom_call" | custom-call | tf_op jit(solution)/shard_map/pallas_call | solution.py:193
Async XLA Ops:
  0.6 39.7 %copy-start = (f32[1024]{0:T(1024)S(1)}, f32[1024]{0:T(1024)}, u32[]{:S(2)}) copy-start(f32[1024]{0:T(1024)} %param.7) | copy-start | bytes 12292

commit v5 on v4

--- a/solution.py
+++ b/solution.py
@@ -21,18 +21,47 @@
     ]
 
 
+NETWORKS = {
+    4: ((0, 1), (2, 3), (0, 2), (1, 3), (1, 2)),
+    8: (
+        (0, 1), (2, 3), (4, 5), (6, 7), (0, 2), (1, 3), (4, 6), (5, 7), (1, 2), (5, 6),
+        (0, 4), (1, 5), (2, 6), (3, 7), (2, 4), (3, 5), (1, 2), (3, 4), (5, 6),
+    ),
+}
+
+
+def lanes_sorted(values):
+    rows = [values[r : r + 1, :] for r in range(values.shape[0])]
+    for a, b in NETWORKS[len(rows)]:
+        rows[a], rows[b] = jnp.maximum(rows[a], rows[b]), jnp.minimum(rows[a], rows[b])
+    return rows
+
+
+def count_above(rows, block):
+    *rows, least = rows
+    if len(rows) == 3:
+        high = rows[1] > block
+        low = jnp.where(high, rows[2], rows[0]) > block
+        count = jnp.where(high, 2.0, 0.0) + jnp.where(low, 1.0, 0.0)
+    else:
+        high = rows[3] > block
+        middle = jnp.where(high, rows[5], rows[1]) > block
+        upper, lower = jnp.where(high, rows[6], rows[2]), jnp.where(high, rows[4], rows[0])
+        low = jnp.where(middle, upper, lower) > block
+        count = (
+            jnp.where(high, 4.0, 0.0) + jnp.where(middle, 2.0, 0.0) + jnp.where(low, 1.0, 0.0)
+        )
+    return count + jnp.where(least > block, 1.0, 0.0)
+
+
 def ranked(values, place):
-    n = values.shape[0]
-    above = [jnp.zeros((8, LANES), jnp.float32) for _ in range(n)]
-    for block in column_blocks(values):
-        for r in range(n):
-            larger = jnp.where(block > values[r : r + 1, :], 1.0, 0.0)
-            above[r] = above[r] + larger.reshape(LANES // 8, 8, LANES).sum(axis=0)
-    best = jnp.full((LANES, LANES), jnp.inf, jnp.float32)
-    for r in range(n):
-        count = above[r].sum(axis=0, keepdims=True)
-        best = jnp.minimum(best, jnp.where(count <= place, values[r : r + 1, :], jnp.inf))
-    return best.T.min(axis=0, keepdims=True)
+    rows = lanes_sorted(values)
+    best = jnp.full((8, LANES), jnp.inf, jnp.float32)
+    for block in column_blocks(jnp.concatenate(rows, axis=0)):
+        above = count_above(rows, block).sum(axis=1, keepdims=True)
+        found = jnp.where(above <= place, block, jnp.inf)
+        best = jnp.minimum(best, found.reshape(LANES // 8, 8, LANES).min(axis=0))
+    return best.min(axis=0, keepdims=True)
 
 
 def scores_kernel(
@@ -101,9 +130,9 @@
 def gather_kernel(n_cand, partial_ref, best_ref, gains_ref, out_ref):
     gains = partial_ref[...].sum(axis=0)
     gains_ref[...] = gains
-    row = lax.broadcasted_iota(jnp.int32, (LANES, LANES), 0)
+    lane = lax.broadcasted_iota(jnp.int32, (1, LANES), 1)
     falling = lax.axis_index("cand") % 2 == 0
-    top = ranked(gains, jnp.where(falling, row, TOPK - 1 - row).astype(jnp.float32))
+    top = ranked(gains, jnp.where(falling, lane, TOPK - 1 - lane).astype(jnp.float32))
     for i in range(n_cand):
         out_ref[i, :, 0:LANES] = top
         out_ref[i, :, LANES:] = best_ref[...]
@@ -122,7 +151,7 @@
     left, right = (jnp.concatenate(half, axis=0) for half in (pairs[0::2], pairs[1::2]))
     lane = lax.broadcasted_iota(jnp.int32, left.shape, 1)
     tops = jnp.where(lane < TOPK, left, pltpu.roll(right, TOPK, 1))
-    place = lax.broadcasted_iota(jnp.int32, (LANES, LANES), 0).astype(jnp.float32)
+    place = lax.broadcasted_iota(jnp.int32, (1, LANES), 1).astype(jnp.float32)
     top_out[...] = ranked(tops, place)[:, 0:TOPK]
 
 

time: 41.6 us -> 41.4 us (level)
  no operation moved by 1% of the time
where the time goes in v5:
time: 41.4 us; the launch traced here: 41.2 us
  blocking collectives  34.1 us (82%)
  Pallas kernels  6.48 us (16%)
  between operations  0.65 us (2%)
    all_to_all x2, blocking collectives, exchanged(): lax.all_to_all(x, axis, split_axis=0, concat_axis=0, axis_index_groups=me...  34.1 us
    pallas_call x1, Pallas kernels, on_device(): pl.pallas_call(functools.partial(scores_kernel, scale, float(local * n_pt...  4.88 us
    pallas_call x1, Pallas kernels, on_device(): pl.pallas_call(final_kernel, out_shape=(jax.ShapeDtypeStruct((rows, LANES...  1.04 us

profile of v5, /device:TPU:1, one launch (start us, length us, event | category | flops | bytes accessed | tf_op | source)
XLA Modules:
  0.0 41.2 jit_solution(2941148975948417177)
XLA Ops:
  0.6 0.0 copy-start
  0.6 4.9 %shard_map.76 = (f32[32,8,128]{2,1,0:T(8,128)S(1)}, f32[1,1024]{1,0:T(1,128)S(1)}) custom-call(s32[64]{0:T(128)} %picks_hbm.1, f32[8,128]{1,0:T(8,128)} %bitcast.8, f32[8,128]{1,0:T(8,128)} %bitcast.6, bf16[1024,1024]{1,0:T(8,128)(2,1)} %points_hbm.1, bf16[1024,1024]{1,0:T(8,128)(2,1)} %cands_hbm.1), custom_call_target="tpu_custom_call" | custom-call | flops 2147483648 | bytes 4194304 | tf_op jit(solution)/shard_map/pallas_call | solution.py:176
  5.5 16.1 %all_to_all.10.partial_ref = f32[32,8,128]{2,1,0:T(8,128)S(1)} all-to-all(f32[32,8,128]{2,1,0:T(8,128)S(1)} %get-tuple-element.10), channel_id=1, replica_groups={{336,352,368,384,400,416,432,448,464,480,496,0,16,32,48,64,80,96,112,12..., dimensions={0} | all-to-all | bytes 262144 | tf_op jit(solution)/shard_map/all_to_all | solution.py:161
  21.7 0.6 %shard_map.77 = (f32[8,128]{1,0:T(8,128)S(1)}, f32[16,1,1152]{2,1,0:T(1,128)S(1)}) custom-call(f32[32,8,128]{2,1,0:T(8,128)S(1)} %all_to_all.10.partial_ref, f32[1,1024]{1,0:T(1,128)S(1)} %get-tuple-element.11.best_ref), custom_call_target="tpu_custom_call" | custom-call | tf_op jit(solution)/shard_map/pallas_call | solution.py:209
  22.2 18.0 %all_to_all.11.all_ref = f32[16,1,1152]{2,1,0:T(1,128)S(1)} all-to-all(f32[16,1,1152]{2,1,0:T(1,128)S(1)} %get-tuple-element.12), channel_id=1, replica_groups={{11,12,13,14,15,0,1,2,3,4,5,6,7,8,9,10},{27,28,29,30,31,16,17,18,19,20,..., dimensions={0} | all-to-all | bytes 147456 | tf_op jit(solution)/shard_map/all_to_all | solution.py:161
  40.2 0.0 copy-done
  40.2 1.0 %shard_map.78 = (f32[8,128]{1,0:T(8,128)}, f32[1,64]{1,0:T(1,128)}, f32[1,1024]{1,0:T(1,128)}) custom-call(f32[16,1,1152]{2,1,0:T(1,128)S(1)} %all_to_all.11.all_ref, f32[1,1024]{1,0:T(1,128)S(1)} %bitcast.7, f32[8,128]{1,0:T(8,128)S(1)} %get-tuple-element.13.gains_ref), custom_call_target="tpu_custom_call" | custom-call | tf_op jit(solution)/shard_map/pallas_call | solution.py:222
Async XLA Ops:
  0.6 39.6 %copy-start = (f32[1024]{0:T(1024)S(1)}, f32[1024]{0:T(1024)}, u32[]{:S(2)}) copy-start(f32[1024]{0:T(1024)} %param.7) | copy-start | bytes 12292
